TPU v7x, 32 devices: a whole 2x2x4 slice. The times are simulated.
32 devices in a mesh: dp: 4 (over y, core), tensor: 8 (over z, x).
Axes of the slice: x: 2, y: 2, z: 4, core: 2. Of those that a mesh axis runs over, the one named last changes fastest.
Arguments:
- attn_input: bfloat16 [512, 8192], P('dp'), may hold values from -6 to 6
- residual: bfloat16 [512, 8192], P('dp'), may hold values from -3 to 3
- query_weight: bfloat16 [8192, 2048], P('dp', 'tensor'), may hold values from -0.0625 to 0.0625
- query_bias: bfloat16 [2048], P('tensor'), may hold values from -3 to 3
- output_weight: bfloat16 [2048, 8192], P('tensor', 'dp'), may hold values from -0.125 to 0.125
- cached_keys: bfloat16 [4, 8, 1024, 128], P('dp', 'tensor'), may hold values from -305 to 305, as said below
- cached_values: bfloat16 [4, 8, 1024, 128], P('dp', 'tensor'), may hold values from -12 to 12, as said below
- norm_gain: bfloat16 [8192], replicated, may hold values from 0.5 to 1.5
Outputs:
- hidden_out: bfloat16 [512, 8192], P(('dp', 'tensor'))
- normed_out: bfloat16 [512, 8192], P('dp')
Inputs may be any that keep to these rules, and one draw needn't show every extreme that they name: `cached_keys`: groups g and g2 with g // 1 == g2 // 1 carry equal keys. `cached_values`: groups g and g2 with g // 1 == g2 // 1 carry equal values.
All inputs are finite; a program needn't handle non-finite values.
Results may differ from a plain program's by a relative error of at most 0.025.
Values may be sent and summed in bfloat16 or wider, within the bound.
No kernel may reach another device: no remote copies, remote signals or barrier semaphores. Data moves between devices by JAX's collectives and lax.ppermute only.
A program may use at most 64 MiB of HBM per device.

v0:
```python
import jax
import jax.numpy as jnp
from jax import lax
from jax.sharding import PartitionSpec as P

rope_theta = 1000000.0
norm_eps = 1e-06


def rotate(projected, first_pos):
    head_dim = projected.shape[-1]
    half_dim = head_dim // 2
    inv_freq = jnp.power(
        jnp.float32(rope_theta), -2.0 * jnp.arange(half_dim, dtype=jnp.float32) / head_dim
    )
    positions = first_pos + jnp.arange(projected.shape[0], dtype=jnp.float32)
    angles = positions[:, None] * inv_freq[None, :]
    cosine = jnp.cos(angles)[:, None, :]
    sine = jnp.sin(angles)[:, None, :]
    first_half = projected[..., :half_dim]
    second_half = projected[..., half_dim:]
    return jnp.concatenate(
        [first_half * cosine - second_half * sine, second_half * cosine + first_half * sine],
        axis=-1,
    )


def attend(queries, local_keys, local_values):
    count_q = queries.shape[0]
    count_k = local_keys.shape[0]
    scores = jnp.einsum("thd,kd->htk", queries, local_keys, preferred_element_type=jnp.float32) * (
        1.0 / queries.shape[-1] ** 0.5
    )
    visible = jnp.arange(count_k)[None, :] <= (count_k - count_q + jnp.arange(count_q))[:, None]
    scores = jnp.where(visible[None], scores, jnp.float32(-1e30))
    highest = jnp.max(scores, axis=-1, keepdims=True)
    expo = jnp.exp(scores - highest)
    soft = (expo / jnp.sum(expo, axis=-1, keepdims=True)).astype(jnp.bfloat16)
    mixed = jnp.einsum("htk,kd->thd", soft, local_values, preferred_element_type=jnp.float32)
    return mixed.astype(jnp.bfloat16)


def normalize(total, norm_gain):
    mean_square = jnp.mean(total * total, axis=-1, keepdims=True)
    return (total * lax.rsqrt(mean_square + norm_eps) * norm_gain.astype(jnp.float32)).astype(
        jnp.bfloat16
    )


def body(
    attn_input,
    residual,
    query_weight,
    query_bias,
    output_weight,
    cached_keys,
    cached_values,
    norm_gain,
):
    tok_count = attn_input.shape[0]
    ctx_len = cached_keys.shape[2]
    head_dim = cached_keys.shape[3]
    local_heads = query_weight.shape[1] // head_dim
    projected = jnp.dot(
        attn_input,
        lax.all_gather(query_weight, "dp", axis=0, tiled=True),
        preferred_element_type=jnp.float32,
    )
    projected = projected + query_bias.astype(jnp.float32)
    queries = rotate(
        projected.reshape(tok_count, local_heads, head_dim), float(ctx_len - tok_count)
    ).astype(jnp.bfloat16)
    mixed = attend(queries, cached_keys[0, 0], cached_values[0, 0]).reshape(
        tok_count, local_heads * head_dim
    )
    partial_sum = jnp.dot(
        mixed,
        lax.all_gather(output_weight, "dp", axis=1, tiled=True),
        preferred_element_type=jnp.float32,
    )
    own_count = tok_count // lax.axis_size("tensor")
    own_start = lax.axis_index("tensor") * own_count
    summed = lax.psum(partial_sum.astype(jnp.bfloat16), "tensor").astype(jnp.float32)
    total = residual.astype(jnp.float32) + summed
    normed_out = normalize(total, norm_gain)
    hidden_out = lax.dynamic_slice_in_dim(total, own_start, own_count, 0).astype(jnp.bfloat16)
    return (hidden_out, normed_out)


def solution(mesh):
    return jax.shard_map(
        body,
        mesh=mesh,
        in_specs=(
            P("dp", None),
            P("dp", None),
            P("dp", "tensor"),
            P("tensor"),
            P("tensor", "dp"),
            P("dp", "tensor", None, None),
            P("dp", "tensor", None, None),
            P(),
        ),
        out_specs=(P(("dp", "tensor"), None), P("dp", None)),
        check_vma=False,
    )
```

profile of v0, /device:TPU:0, one launch (start us, length us, event | category | flops | bytes accessed | tf_op | source)
XLA Modules:
  0.0 202.9 jit_solution(6312552266347994281)
XLA Ops:
  7.2 0.0 copy-start
  7.2 0.0 all-gather.3.cloned.1.call-start
  7.2 0.7 all-gather.3.cloned.1.call-update
  7.9 0.0 all-gather.5.cloned.1.call-start
  8.0 0.7 all-gather.5.cloned.1.call-update
  8.7 0.0 copy-start.3
  8.7 0.0 all-reduce.2.cloned.1.call-start
  8.7 0.7 convert_element_type.32
  9.4 0.1 iota_compare_fusion
  9.6 0.3 multiply_cosine_fusion
  9.9 36.9 %all-gather.3.cloned.1.call-done = bf16[8192,256]{1,0:T(8,128)(2,1)} async-done(((bf16[2048,256]{1,0:T(8,128)(2,1)}), bf16[8192,256]{1,0:T(8,128)(2,1)}) %all-gather.3.cloned.1.call-update) | async-done | bytes 4194320 | tf_op jit(solution)/shard_map/all_gather | solution.py:66
  46.8 0.0 copy-done
  46.8 2.9 %convolution_add_fusion = f32[128,256]{1,0:T(8,128)S(1)} fusion(bf16[128,8192]{1,0:T(8,128)(2,1)S(1)} %copy-done, bf16[8192,256]{1,0:T(8,128)(2,1)} %all-gather.3.cloned.1.call-done, f32[256]{0:T(256)S(1)} %convert_element_type.32), kind=kOutput, calls=%fused_computation.10 | convolution fusion | flops 536903680 | bytes 6423552 | tf_op jit(solution)/shard_map/dot_general | solution.py:64
  49.7 0.1 reshape.101
  49.7 0.2 fusion.15
  50.0 0.0 copy-start.4
  50.0 0.0 copy-start.5
  50.0 0.6 copy-done.4
  50.6 0.0 copy-done.5
  50.7 0.0 copy-done.3
  50.7 0.6 fusion.16
  51.3 1.2 fusion.4
  52.5 1.7 convolution_convert_fusion.1
  54.2 28.6 %all-gather.5.cloned.1.call-done = bf16[256,8192]{1,0:T(8,128)(2,1)} async-done(((bf16[256,2048]{1,0:T(8,128)(2,1)}), bf16[256,8192]{1,0:T(8,128)(2,1)}) %all-gather.5.cloned.1.call-update) | async-done | bytes 4194320 | tf_op jit(solution)/shard_map/all_gather | solution.py:78
  82.8 0.0 copy-start.6
  82.8 4.3 %convolution_convert_fusion = bf16[128,8192]{1,0:T(8,128)(2,1)} fusion(bf16[128,256]{0,1:T(8,128)(2,1)S(1)} %bitcast.28, bf16[256,8192]{1,0:T(8,128)(2,1)} %all-gather.5.cloned.1.call-done), kind=kOutput, calls=%fused_computation.1 | convolution fusion | flops 537919488 | bytes 6356992 | tf_op jit(solution)/shard_map/dot_general | solution.py:76
  87.1 0.0 all-reduce.2.cloned.1.call-update
  87.1 0.0 copy-done.6
  87.1 102.4 %all-reduce.2.cloned.1.call-done = bf16[128,8192]{1,0:T(8,128)(2,1)} async-done(((bf16[128,8192]{1,0:T(8,128)(2,1)}), bf16[128,8192]{1,0:T(8,128)(2,1)}) %all-reduce.2.cloned.1.call-update) | async-done | bytes 2097168 | tf_op jit(solution)/shard_map/psum | solution.py:83
  189.6 0.0 copy-start.1
  189.6 0.0 copy-start.2
  189.6 3.1 %multiply_reduce_fusion = f32[128]{0:T(128)S(1)} fusion(bf16[128,8192]{1,0:T(8,128)(2,1)} %all-reduce.2.cloned.1.call-done, bf16[128,8192]{1,0:T(8,128)(2,1)} %param.9), kind=kLoop, calls=%fused_computation.3 | loop fusion | flops 5242752 | bytes 4194816 | tf_op jit(solution)/shard_map/reduce_sum | solution.py:44
  192.7 0.0 copy-done.1
  192.7 0.3 copy-done.2
  193.0 0.5 convert_add_fusion
  193.5 0.7 dynamic-slice_convert_fusion
  194.3 2.1 %multiply_convert_fusion = bf16[128,8192]{1,0:T(8,128)(2,1)} fusion(f32[8192]{0:T(1024)S(1)} %convert_element_type.39, f32[128]{0:T(128)S(1)} %add_rsqrt_fusion, bf16[128,8192]{1,0:T(8,128)(2,1)S(1)} %copy-done.2, bf16[128,8192]{1,0:T(8,128)(2,1)S(1)} %copy-done.1), kind=kLoop, calls=%fused_computation.2 | loop fusion | flops 6291456 | bytes 6324736 | tf_op jit(solution)/shard_map/convert_element_type | solution.py:45
  (6 shorter events, 0.1 us)
Async XLA Ops:
  7.2 39.6 %copy-start = (bf16[128,8192]{1,0:T(8,128)(2,1)S(1)}, bf16[128,8192]{1,0:T(8,128)(2,1)}, u32[]{:S(2)}) copy-start(bf16[128,8192]{1,0:T(8,128)(2,1)} %param.8) | copy-start | bytes 6291460
  7.2 39.6 %all-gather.3.cloned.1.call-start = ((), (), s32[]{:S(2)}) async-start(), calls=%async_computation | async-start | bytes 5242880 | tf_op jit(solution)/shard_map/all_gather | solution.py:66
  7.9 74.9 %all-gather.5.cloned.1.call-start = ((), (), s32[]{:S(2)}) async-start(), calls=%async_computation.1 | async-start | bytes 5242880 | tf_op jit(solution)/shard_map/all_gather | solution.py:78
  8.7 42.0 %copy-start.3 = (bf16[1,1,1024,128]{3,2,1,0:T(8,128)(2,1)S(1)}, bf16[1,1,1024,128]{3,2,1,0:T(8,128)(2,1)}, u32[]{:S(2)}) copy-start(bf16[1,1,1024,128]{3,2,1,0:T(8,128)(2,1)} %param.13) | copy-start | bytes 786436
  8.7 180.9 %all-reduce.2.cloned.1.call-start = ((), (), s32[]{:S(2)}) async-start(), calls=%async_computation.2 | async-start | bytes 4194304 | tf_op jit(solution)/shard_map/psum | solution.py:83
  50.0 0.6 copy-start.4
  50.0 0.6 copy-start.5
  82.8 4.3 %copy-start.6 = (bf16[8192]{0:T(1024)(128)(2,1)S(1)}, bf16[8192]{0:T(1024)(128)(2,1)}, u32[]{:S(2)}) copy-start(bf16[8192]{0:T(1024)(128)(2,1)} %param.15) | copy-start | bytes 49156
  189.6 3.2 %copy-start.1 = (bf16[128,8192]{1,0:T(8,128)(2,1)S(1)}, bf16[128,8192]{1,0:T(8,128)(2,1)}, u32[]{:S(2)}) copy-start(bf16[128,8192]{1,0:T(8,128)(2,1)} %param.9) | copy-start | bytes 6291460
  189.6 3.5 %copy-start.2 = (bf16[128,8192]{1,0:T(8,128)(2,1)S(1)}, bf16[128,8192]{1,0:T(8,128)(2,1)}, u32[]{:S(2)}) copy-start(bf16[128,8192]{1,0:T(8,128)(2,1)} %all-reduce.2.cloned.1.call-done) | copy-start | bytes 6291460
Sparse Core Ops, SparseCore 0:
  9.5 37.1 all-gather.2
  48.3 34.4 all-gather.4
  87.2 102.2 all-reduce.1
where the time goes:
time: 203 us
  waiting for transfers between devices  169 us (83%)
  between operations  13.9 us (7%)
  matrix products  10.7 us (5%)
  other arithmetic  6.93 us (3%)
    psum x1, waiting for transfers between devices, body(): lax.psum(partial_sum.astype(jnp.bfloat16), 'tensor').astype(jnp.float32)  102 us
    all_gather x1, waiting for transfers between devices, body(): lax.all_gather(query_weight, 'dp', axis=0, tiled=True)  36.9 us
    all_gather x1, waiting for transfers between devices, body(): lax.all_gather(output_weight, 'dp', axis=1, tiled=True)  28.6 us
    dot_general x1, matrix products, body(): jnp.dot(mixed, lax.all_gather(output_weight, 'dp', axis=1, tiled=True), p...  4.27 us
  transfers between devices with their start and end apart: 3, of which 3 were waited for; matrix products, arithmetic and copies ran while one was open for 4% of the time, Pallas kernels for 0%

commit v1 on v0

--- a/solution.py
+++ b/solution.py
@@ -5,6 +5,12 @@
 
 rope_theta = 1000000.0
 norm_eps = 1e-06
+
+
+def stack_and_merge(x, axis, along):
+    parts = lax.all_gather(x, axis, axis=0, tiled=False)
+    whole = jnp.concatenate(parts, axis=along)
+    return whole
 
 
 def rotate(projected, first_pos):
@@ -74,9 +80,7 @@
         tok_count, local_heads * head_dim
     )
     partial_sum = jnp.dot(
-        mixed,
-        lax.all_gather(output_weight, "dp", axis=1, tiled=True),
-        preferred_element_type=jnp.float32,
+        mixed, stack_and_merge(output_weight, "dp", 1), preferred_element_type=jnp.float32
     )
     own_count = tok_count // lax.axis_size("tensor")
     own_start = lax.axis_index("tensor") * own_count

time: 203 us -> 211 us (1.039)
  local copies, waits for them, and re-layouts: 1.98 us -> 8.27 us
    reshape x0 -> x1, local copies, waits for them, and re-layouts: none -> 6.29 us  [stack_and_merge(): whole = jnp.concatenate(parts, axis=along)]
  transfers between devices with their start and end apart: 3 -> 3, of which waited for: 3 -> 3; matrix products, arithmetic and copies ran while one was open for 4% -> 3% of each run, Pallas kernels for 0% -> 0%
where the time goes in v1:
time: 211 us
  waiting for transfers between devices  171 us (81%)
  between operations  13.9 us (7%)
  matrix products  10.5 us (5%)
  local copies, waits for them, and re-layouts  8.27 us (4%)
  other arithmetic  6.93 us (3%)
    psum x1, waiting for transfers between devices, body(): lax.psum(partial_sum.astype(jnp.bfloat16), 'tensor').astype(jnp.float32)  102 us
    all_gather x1, waiting for transfers between devices, body(): lax.all_gather(query_weight, 'dp', axis=0, tiled=True)  36.9 us
    all_gather x1, waiting for transfers between devices, stack_and_merge(): parts = lax.all_gather(x, axis, axis=0, tiled=False)  30.3 us
    reshape x1, local copies, waits for them, and re-layouts, stack_and_merge(): whole = jnp.concatenate(parts, axis=along)  6.29 us
    dot_general x1, matrix products, body(): jnp.dot(mixed, stack_and_merge(output_weight, 'dp', 1), preferred_element...  5.01 us
  transfers between devices with their start and end apart: 3, of which 3 were waited for; matrix products, arithmetic and copies ran while one was open for 3% of the time, Pallas kernels for 0%

profile of v1, /device:TPU:0, one launch (start us, length us, event | category | flops | bytes accessed | tf_op | source)
XLA Modules:
  0.0 210.6 jit_solution(11857248919753665595)
XLA Ops:
  7.2 0.0 copy-start
  7.2 0.0 all-gather.4.cloned.1.call-start
  7.2 0.7 all-gather.4.cloned.1.call-update
  7.9 0.0 all-gather.6.cloned.1.call-start
  8.0 0.7 all-gather.6.cloned.1.call-update
  8.7 0.0 copy-start.3
  8.7 0.0 all-reduce.2.cloned.1.call-start
  8.7 0.7 convert_element_type.32
  9.4 0.1 iota_compare_fusion
  9.6 0.3 multiply_cosine_fusion
  9.9 36.9 %all-gather.4.cloned.1.call-done = bf16[8192,256]{1,0:T(8,128)(2,1)} async-done(((bf16[2048,256]{1,0:T(8,128)(2,1)}), bf16[8192,256]{1,0:T(8,128)(2,1)}) %all-gather.4.cloned.1.call-update) | async-done | bytes 4194320 | tf_op jit(solution)/shard_map/all_gather | solution.py:72
  46.8 0.0 copy-done
  46.8 2.9 %convolution_add_fusion = f32[128,256]{1,0:T(8,128)S(1)} fusion(bf16[128,8192]{1,0:T(8,128)(2,1)S(1)} %copy-done, bf16[8192,256]{1,0:T(8,128)(2,1)} %all-gather.4.cloned.1.call-done, f32[256]{0:T(256)S(1)} %convert_element_type.32), kind=kOutput, calls=%fused_computation.10 | convolution fusion | flops 536903680 | bytes 6423552 | tf_op jit(solution)/shard_map/dot_general | solution.py:70
  49.7 0.1 reshape.107
  49.7 0.2 fusion.15
  50.0 0.0 copy-start.4
  50.0 0.0 copy-start.5
  50.0 0.6 copy-done.4
  50.6 0.0 copy-done.5
  50.7 0.0 copy-done.3
  50.7 0.6 fusion.16
  51.3 1.2 fusion.4
  52.5 30.3 %all-gather.6.cloned.1.call-done = bf16[1024,2048]{1,0:T(8,128)(2,1)} async-done(((bf16[256,2048]{1,0:T(8,128)(2,1)}), bf16[1024,2048]{1,0:T(8,128)(2,1)}) %all-gather.6.cloned.1.call-update) | async-done | bytes 4194320 | tf_op jit(solution)/shard_map/all_gather | solution.py:11
  82.8 0.0 copy-start.7
  82.8 6.3 %copy.19 = bf16[256,4,2048]{0,2,1:T(8,128)(2,1)} copy(bf16[256,4,2048]{2,0,1:T(8,128)(2,1)} %bitcast.33) | data formatting | bytes 8388608 | tf_op jit(solution)/shard_map/reshape | solution.py:12
  89.1 0.0 copy-done.7
  89.1 0.7 convolution_convert_fusion.1
  89.8 0.0 copy-start.6
  89.8 5.0 %convolution_convert_fusion = bf16[128,8192]{1,0:T(8,128)(2,1)} fusion(bf16[128,256]{0,1:T(8,128)(2,1)S(1)} %bitcast.34, bf16[256,8192]{0,1:T(8,128)(2,1)} %bitcast.32), kind=kOutput, calls=%fused_computation.1 | convolution fusion | flops 537919488 | bytes 6356992 | tf_op jit(solution)/shard_map/dot_general | solution.py:82
  94.8 0.0 all-reduce.2.cloned.1.call-update
  94.9 0.0 copy-done.6
  94.9 102.4 %all-reduce.2.cloned.1.call-done = bf16[128,8192]{1,0:T(8,128)(2,1)} async-done(((bf16[128,8192]{1,0:T(8,128)(2,1)}), bf16[128,8192]{1,0:T(8,128)(2,1)}) %all-reduce.2.cloned.1.call-update) | async-done | bytes 2097168 | tf_op jit(solution)/shard_map/psum | solution.py:87
  197.3 0.0 copy-start.1
  197.3 0.0 copy-start.2
  197.3 3.1 %multiply_reduce_fusion = f32[128]{0:T(128)S(1)} fusion(bf16[128,8192]{1,0:T(8,128)(2,1)} %all-reduce.2.cloned.1.call-done, bf16[128,8192]{1,0:T(8,128)(2,1)} %param.9), kind=kLoop, calls=%fused_computation.3 | loop fusion | flops 5242752 | bytes 4194816 | tf_op jit(solution)/shard_map/reduce_sum | solution.py:50
  200.4 0.0 copy-done.1
  200.5 0.3 copy-done.2
  200.8 0.5 convert_add_fusion
  201.3 0.7 dynamic-slice_convert_fusion
  202.0 2.1 multiply_convert_fusion
  (6 shorter events, 0.1 us)
Async XLA Ops:
  7.2 39.6 %copy-start = (bf16[128,8192]{1,0:T(8,128)(2,1)S(1)}, bf16[128,8192]{1,0:T(8,128)(2,1)}, u32[]{:S(2)}) copy-start(bf16[128,8192]{1,0:T(8,128)(2,1)} %param.8) | copy-start | bytes 6291460
  7.2 39.6 %all-gather.4.cloned.1.call-start = ((), (), s32[]{:S(2)}) async-start(), calls=%async_computation | async-start | bytes 5242880 | tf_op jit(solution)/shard_map/all_gather | solution.py:72
  7.9 74.9 %all-gather.6.cloned.1.call-start = ((), (), s32[]{:S(2)}) async-start(), calls=%async_computation.2 | async-start | bytes 5242880 | tf_op jit(solution)/shard_map/all_gather | solution.py:11
  8.7 42.0 %copy-start.3 = (bf16[1,1,1024,128]{3,2,1,0:T(8,128)(2,1)S(1)}, bf16[1,1,1024,128]{3,2,1,0:T(8,128)(2,1)}, u32[]{:S(2)}) copy-start(bf16[1,1,1024,128]{3,2,1,0:T(8,128)(2,1)} %param.13) | copy-start | bytes 786436
  8.7 188.6 %all-reduce.2.cloned.1.call-start = ((), (), s32[]{:S(2)}) async-start(), calls=%async_computation.1 | async-start | bytes 4194304 | tf_op jit(solution)/shard_map/psum | solution.py:87
  50.0 0.6 copy-start.4
  50.0 0.6 copy-start.5
  82.8 6.3 %copy-start.7 = (bf16[1,1,1024,128]{3,2,1,0:T(8,128)(2,1)S(1)}, bf16[1,1,1024,128]{3,2,1,0:T(8,128)(2,1)}, u32[]{:S(2)}) copy-start(bf16[1,1,1024,128]{3,2,1,0:T(8,128)(2,1)} %param.14) | copy-start | bytes 786436
  89.8 5.1 %copy-start.6 = (bf16[8192]{0:T(1024)(128)(2,1)S(1)}, bf16[8192]{0:T(1024)(128)(2,1)}, u32[]{:S(2)}) copy-start(bf16[8192]{0:T(1024)(128)(2,1)} %param.15) | copy-start | bytes 49156
  197.3 3.2 %copy-start.1 = (bf16[128,8192]{1,0:T(8,128)(2,1)S(1)}, bf16[128,8192]{1,0:T(8,128)(2,1)}, u32[]{:S(2)}) copy-start(bf16[128,8192]{1,0:T(8,128)(2,1)} %param.9) | copy-start | bytes 6291460
  197.3 3.5 %copy-start.2 = (bf16[128,8192]{1,0:T(8,128)(2,1)S(1)}, bf16[128,8192]{1,0:T(8,128)(2,1)}, u32[]{:S(2)}) copy-start(bf16[128,8192]{1,0:T(8,128)(2,1)} %all-reduce.2.cloned.1.call-done) | copy-start | bytes 6291460
Sparse Core Ops, SparseCore 0:
  9.5 37.1 all-gather.3
  48.3 34.4 all-gather.5
  95.0 102.2 all-reduce.1

commit v2 on v0

--- a/solution.py
+++ b/solution.py
@@ -5,6 +5,12 @@
 
 rope_theta = 1000000.0
 norm_eps = 1e-06
+
+
+def add_all(x, name):
+    terms = lax.all_gather(x, name, axis=0, tiled=False)
+    result = terms.sum(axis=0)
+    return result
 
 
 def rotate(projected, first_pos):
@@ -80,7 +86,7 @@
     )
     own_count = tok_count // lax.axis_size("tensor")
     own_start = lax.axis_index("tensor") * own_count
-    summed = lax.psum(partial_sum.astype(jnp.bfloat16), "tensor").astype(jnp.float32)
+    summed = add_all(partial_sum.astype(jnp.bfloat16), "tensor").astype(jnp.float32)
     total = residual.astype(jnp.float32) + summed
     normed_out = normalize(total, norm_gain)
     hidden_out = lax.dynamic_slice_in_dim(total, own_start, own_count, 0).astype(jnp.bfloat16)

time: 203 us -> 339 us (1.67)
  waiting for transfers between devices: 169 us -> 294 us
  other arithmetic: 6.93 us -> 17.4 us
    all_gather x0 -> x1, waiting for transfers between devices: none -> 227 us  [add_all(): terms = lax.all_gather(x, name, axis=0, tiled=False)]
    psum x1 -> x0, waiting for transfers between devices: 102 us -> none  [body(): lax.psum(partial_sum.astype(jnp.bfloat16), 'tensor').astype(jnp.float32)]
    reduce_sum x0 -> x1, other arithmetic: none -> 10.5 us  [add_all(): result = terms.sum(axis=0)]
  transfers between devices with their start and end apart: 3 -> 3, of which waited for: 3 -> 3; matrix products, arithmetic and copies ran while one was open for 4% -> 2% of each run, Pallas kernels for 0% -> 0%
where the time goes in v2:
time: 339 us; the launch traced here: 338 us
  waiting for transfers between devices  294 us (87%)
  other arithmetic  17.4 us (5%)
  between operations  13.9 us (4%)
  matrix products  10.7 us (3%)
    all_gather x1, waiting for transfers between devices, add_all(): terms = lax.all_gather(x, name, axis=0, tiled=False)  227 us
    all_gather x1, waiting for transfers between devices, body(): lax.all_gather(query_weight, 'dp', axis=0, tiled=True)  36.9 us
    all_gather x1, waiting for transfers between devices, body(): lax.all_gather(output_weight, 'dp', axis=1, tiled=True)  28.6 us
    reduce_sum x1, other arithmetic, add_all(): result = terms.sum(axis=0)  10.5 us
  transfers between devices with their start and end apart: 3, of which 3 were waited for; matrix products, arithmetic and copies ran while one was open for 2% of the time, Pallas kernels for 0%

profile of v2, /device:TPU:0, one launch (start us, length us, event | category | flops | bytes accessed | tf_op | source)
XLA Modules:
  0.0 338.3 jit_solution(11752251626231080506)
XLA Ops:
  7.2 0.0 copy-start
  7.2 0.0 all-gather.5.cloned.1.call-start
  7.2 0.7 all-gather.5.cloned.1.call-update
  7.9 0.0 all-gather.7.cloned.1.call-start
  8.0 0.7 all-gather.7.cloned.1.call-update
  8.7 0.0 copy-start.3
  8.7 0.0 all-gather.9.cloned.1.call-start
  8.7 0.7 convert_element_type.34
  9.4 0.1 iota_compare_fusion
  9.6 0.3 multiply_cosine_fusion
  9.9 36.9 %all-gather.5.cloned.1.call-done = bf16[8192,256]{1,0:T(8,128)(2,1)} async-done(((bf16[2048,256]{1,0:T(8,128)(2,1)}), bf16[8192,256]{1,0:T(8,128)(2,1)}) %all-gather.5.cloned.1.call-update) | async-done | bytes 4194320 | tf_op jit(solution)/shard_map/all_gather | solution.py:72
  46.8 0.0 copy-done
  46.8 2.9 convolution_add_fusion
  49.7 0.1 reshape.101
  49.7 0.2 fusion.15
  50.0 0.0 copy-start.4
  50.0 0.0 copy-start.5
  50.0 0.6 copy-done.4
  50.6 0.0 copy-done.5
  50.7 0.0 copy-done.3
  50.7 0.6 fusion.16
  51.3 1.2 fusion.4
  52.5 1.7 convolution_convert_fusion.1
  54.2 28.6 %all-gather.7.cloned.1.call-done = bf16[256,8192]{1,0:T(8,128)(2,1)} async-done(((bf16[256,2048]{1,0:T(8,128)(2,1)}), bf16[256,8192]{1,0:T(8,128)(2,1)}) %all-gather.7.cloned.1.call-update) | async-done | bytes 4194320 | tf_op jit(solution)/shard_map/all_gather | solution.py:84
  82.8 0.0 copy-start.6
  82.8 4.3 %convolution_convert_fusion = bf16[128,8192]{1,0:T(8,128)(2,1)} fusion(bf16[128,256]{0,1:T(8,128)(2,1)S(1)} %bitcast.30, bf16[256,8192]{1,0:T(8,128)(2,1)} %all-gather.7.cloned.1.call-done), kind=kOutput, calls=%fused_computation.1 | convolution fusion | flops 537919488 | bytes 6356992 | tf_op jit(solution)/shard_map/dot_general | solution.py:82
  87.1 0.0 all-gather.9.cloned.1.call-update
  87.1 0.0 copy-done.6
  87.1 227.4 %all-gather.9.cloned.1.call-done = bf16[1024,8192]{1,0:T(8,128)(2,1)} async-done(((bf16[128,8192]{1,0:T(8,128)(2,1)}), bf16[1024,8192]{1,0:T(8,128)(2,1)}) %all-gather.9.cloned.1.call-update) | async-done | bytes 16777232 | tf_op jit(solution)/shard_map/all_gather | solution.py:11
  314.5 10.5 %reduce_sum.31 = bf16[128,8192]{1,0:T(8,128)(2,1)} reduce(bf16[8,128,8192]{2,1,0:T(8,128)(2,1)} %bitcast.29, bf16[]{:T(256)} %constant.12.clone.1), dimensions={0}, to_apply=%region_2.3 | reduce | flops 7340032 | bytes 18874370 | tf_op jit(solution)/shard_map/reduce_sum | solution.py:12
  325.0 0.0 copy-start.1
  325.0 0.0 copy-start.2
  325.0 3.1 multiply_reduce_fusion
  328.1 0.0 copy-done.1
  328.2 0.3 copy-done.2
  328.5 0.5 convert_add_fusion
  329.0 2.1 multiply_convert_fusion
  331.1 0.7 dynamic-slice_convert_fusion
  (6 shorter events, 0.1 us)
Async XLA Ops:
  7.2 39.6 %copy-start = (bf16[128,8192]{1,0:T(8,128)(2,1)S(1)}, bf16[128,8192]{1,0:T(8,128)(2,1)}, u32[]{:S(2)}) copy-start(bf16[128,8192]{1,0:T(8,128)(2,1)} %param.8) | copy-start | bytes 6291460
  7.2 39.6 %all-gather.5.cloned.1.call-start = ((), (), s32[]{:S(2)}) async-start(), calls=%async_computation | async-start | bytes 5242880 | tf_op jit(solution)/shard_map/all_gather | solution.py:72
  7.9 74.9 %all-gather.7.cloned.1.call-start = ((), (), s32[]{:S(2)}) async-start(), calls=%async_computation.1 | async-start | bytes 5242880 | tf_op jit(solution)/shard_map/all_gather | solution.py:84
  8.7 42.0 %copy-start.3 = (bf16[1,1,1024,128]{3,2,1,0:T(8,128)(2,1)S(1)}, bf16[1,1,1024,128]{3,2,1,0:T(8,128)(2,1)}, u32[]{:S(2)}) copy-start(bf16[1,1,1024,128]{3,2,1,0:T(8,128)(2,1)} %param.13) | copy-start | bytes 786436
  8.7 305.9 %all-gather.9.cloned.1.call-start = ((), (), s32[]{:S(2)}) async-start(), calls=%async_computation.2 | async-start | bytes 18874368 | tf_op jit(solution)/shard_map/all_gather | solution.py:11
  50.0 0.6 copy-start.4
  50.0 0.6 copy-start.5
  82.8 4.3 %copy-start.6 = (bf16[8192]{0:T(1024)(128)(2,1)S(1)}, bf16[8192]{0:T(1024)(128)(2,1)}, u32[]{:S(2)}) copy-start(bf16[8192]{0:T(1024)(128)(2,1)} %param.15) | copy-start | bytes 49156
  325.0 3.1 copy-start.1
  325.0 3.5 %copy-start.2 = (bf16[128,8192]{1,0:T(8,128)(2,1)S(1)}, bf16[128,8192]{1,0:T(8,128)(2,1)}, u32[]{:S(2)}) copy-start(bf16[128,8192]{1,0:T(8,128)(2,1)} %param.9) | copy-start | bytes 6291460
Sparse Core Ops, SparseCore 0:
  9.5 37.1 all-gather.4
  48.3 34.4 all-gather.6
  87.2 227.2 all-gather.8
